TPU v7x, 32 devices: a whole 2x2x4 slice. The times are simulated.
32 devices in a mesh: hi: 4 (over y, core), lo: 8 (over z, x).
Axes of the slice: x: 2, y: 2, z: 4, core: 2. Of those that a mesh axis runs over, the one named last changes fastest.
Arguments:
- grm: bfloat16 [4, 8, 64, 4, 512], P(None, 'lo', None, 'hi'), as said below
- right_sides: float32 [2048, 512], P(('hi', 'lo')), may hold values from -6 to 6
- inv_diag: float32 [2048], P(('hi', 'lo')), may hold values from 0.3 to 1
- bases: float32 [2048, 576], P(('hi', 'lo')), may hold values from -0.75 to 0.75
- couplings: float32 [9, 64, 64], replicated, as said below
- level_map: int32 [8], replicated, may hold values from 0 to 7, each once
- variance: float32 [2], replicated, may hold values from 0.3 to 1.5
- iters_per_column: int32 [512], replicated, may hold values from 1 to 3
Outputs:
- solution: float32 [2048, 512], P(('hi', 'lo'))
- residual: float32 [2048, 512], P(('hi', 'lo'))
Inputs may be any that keep to these rules, and one draw needn't show every extreme that they name: `grm`: G is symmetric and positive definite. `couplings`: each of the 9 matrices is symmetric and positive definite. `level_map`: a permutation of the levels.
All inputs are finite; a program needn't handle non-finite values.
Results may differ from a plain program's by a relative error of at most 0.0055.
Values may be sent and summed in bfloat16 or wider, within the bound.
A program may use at most 64 MiB of HBM per device.

v0:
```python
import jax
import jax.numpy as jnp
from jax import lax
from jax.sharding import PartitionSpec as P

ITERS = 3


def from_partner(value, axis, bit):
    mask = 2**bit
    pairs = [(source, source ^ mask) for source in range(lax.axis_size(axis))]
    return lax.ppermute(value, axis, pairs)


def level_pieces(coefficients, couplings, level):
    level_ids = jnp.arange(couplings.shape[0], dtype=jnp.int32)
    select = (level_ids == level).astype(jnp.float32)
    own_part = jnp.einsum("l,lrb->rb", select, coefficients)
    matrix = jnp.einsum("l,lrs->rs", select, couplings)
    return (own_part, matrix, select)


def add_level(stacked, own_part, other_part, matrix, select):
    term = jnp.dot(matrix, own_part + other_part, precision=lax.Precision.HIGHEST)
    return stacked + select[:, None, None] * term[None]


def local(grm, right_sides, inv_diag, bases, couplings, level_map, variance, iters_per_column):
    row_count, column_count = right_sides.shape
    grm_block = grm.reshape(-1, grm.shape[4])
    level_total = couplings.shape[0]
    rank_width = couplings.shape[1]
    lo_bits = lax.axis_size("lo").bit_length() - 1
    hi_bits = lax.axis_size("hi").bit_length() - 1
    genetic = variance[0]
    noise = variance[1]

    def precondition(resid):
        coefficients = lax.dot_general(
            bases, resid, (((0,), (0,)), ((), ())), precision=lax.Precision.HIGHEST
        )
        coefficients = coefficients.reshape(level_total, rank_width, column_count)
        stacked = jnp.zeros((level_total - 1, rank_width, column_count), jnp.float32)
        for bit_index in range(lo_bits):
            own_part, matrix, select = level_pieces(coefficients, couplings, level_map[bit_index])
            other_part = from_partner(own_part.astype(jnp.bfloat16), "lo", bit_index).astype(
                own_part.dtype
            )
            stacked = add_level(stacked, own_part, other_part, matrix, select[: level_total - 1])
        for bit_index in range(hi_bits):
            own_part, matrix, select = level_pieces(
                coefficients, couplings, level_map[lo_bits + bit_index]
            )
            other_part = from_partner(own_part.astype(jnp.bfloat16), "hi", bit_index).astype(
                own_part.dtype
            )
            stacked = add_level(stacked, own_part, other_part, matrix, select[: level_total - 1])
        split_at = (level_total - 1) * rank_width
        local_part = inv_diag[:, None] * resid + jnp.dot(
            bases[:, :split_at],
            stacked.reshape(split_at, column_count),
            precision=lax.Precision.HIGHEST,
        )
        coarse_basis = bases[:, split_at:]
        partial_energy = jnp.sum(resid * local_part, axis=0)
        total, summed_energy = lax.psum(
            (coefficients[level_total - 1], partial_energy), ("hi", "lo")
        )
        coarse = jnp.dot(couplings[level_total - 1], total, precision=lax.Precision.HIGHEST)
        scaled = local_part + jnp.dot(coarse_basis, coarse, precision=lax.Precision.HIGHEST)
        energy = summed_energy + jnp.sum(total * coarse, axis=0)
        return (scaled, energy)

    solution = jnp.zeros_like(right_sides)
    residual = right_sides
    scaled, energy = precondition(residual)
    direction = scaled
    for step in range(ITERS):
        rounded = direction.astype(jnp.bfloat16)
        partial_value = jnp.dot(
            grm_block,
            lax.all_gather(rounded, "lo", axis=0, tiled=True),
            preferred_element_type=jnp.float32,
        )
        product = lax.psum_scatter(partial_value, "hi", scatter_dimension=0, tiled=True)
        image = genetic * product + noise * direction
        curvature = lax.psum(jnp.sum(direction * image, axis=0), ("hi", "lo"))
        alpha = energy / curvature
        stepsize = jnp.where(step < iters_per_column, alpha, jnp.zeros_like(alpha))
        solution = solution + stepsize * direction
        residual = residual - stepsize * image
        if step + 1 < ITERS:
            scaled, fresh = precondition(residual)
            direction = scaled + fresh / energy * direction
            energy = fresh
    return (solution, residual)


def solution(mesh):
    in_specs = (
        P(None, "lo", None, "hi", None),
        P(("hi", "lo"), None),
        P(("hi", "lo")),
        P(("hi", "lo"), None),
        P(),
        P(),
        P(),
        P(),
    )
    out_specs = (P(("hi", "lo"), None), P(("hi", "lo"), None))
    return jax.shard_map(local, mesh=mesh, in_specs=in_specs, out_specs=out_specs, check_vma=False)
```

profile of v0, /device:TPU:0, one launch (start us, length us, event | category | flops | bytes accessed | tf_op | source)
XLA Modules:
  0.0 806.3 jit_solution(18174941709177877963)
XLA Ops:
  7.2 1.5 fusion.146
  8.7 2.1 fusion.150
  10.8 1.3 fusion.26
  12.1 3.1 collective-permute-start.1
  15.3 1.4 fusion.24
  16.6 2.7 collective-permute-start.2
  19.3 1.4 fusion.22
  20.8 1.4 fusion.20
  22.1 1.6 collective-permute-start.4
  23.7 1.4 fusion.28
  25.1 1.6 collective-permute-start
  30.6 0.9 fusion.58
  31.5 0.9 fusion.54
  32.4 0.8 fusion.56
  33.3 0.9 fusion.50
  34.2 0.9 fusion.52
  35.8 112.5 %all-reduce.5.cloned.1.call-done = f32[64,512]{1,0:T(8,128)} async-done(((f32[64,512]{1,0:T(8,128)}), f32[64,512]{1,0:T(8,128)}) %all-reduce.5.cloned.1.call-update) | async-done | bytes 131088 | tf_op jit(solution)/shard_map/psum | solution.py:66
  148.4 1.3 fusion.72
  151.6 0.8 multiply_reduce_fusion.5
  152.7 31.3 %all_gather.9 = bf16[512,512]{1,0:T(8,128)(2,1)S(1)} all-gather(bf16[64,512]{1,0:T(8,128)(2,1)S(1)} %get-tuple-element.19), channel_id=1, replica_groups=mesh['hi'=4,'lo'=8] {'lo'}, dimensions={0}, use_global_device_ids=true | all-gather | bytes 589824 | tf_op jit(solution)/shard_map/all_gather | solution.py:82
  184.0 1.1 convolution_bitcast_fusion.2
  185.8 20.3 %reduce-scatter.4.cloned.1.call-done = f32[64,512]{1,0:T(8,128)} async-done(((f32[256,512]{1,0:T(8,128)}), f32[64,512]{1,0:T(8,128)}) %reduce-scatter.4.cloned.1.call-update) | async-done | bytes 131088 | tf_op jit(solution)/shard_map/reduce_scatter | solution.py:85
  206.1 2.2 multiply_reduce_fusion.4
  208.3 39.5 %all-reduce = (f32[512]{0:T(512)S(1)}, f32[512]{0:T(512)S(1)}) all-reduce(f32[512]{0:T(512)S(1)} %get-tuple-element.21, f32[512]{0:T(512)S(1)} %multiply_reduce_fusion.4), channel_id=1, replica_groups=mesh['hi'=4,'lo'=8] {'hi','lo'}, use_global_device_ids=true, to_apply=%region_1.0 | all-reduce | flops 1024 | bytes 8192 | tf_op jit(solution)/shard_map/psum | solution.py:66
  247.8 2.2 multiply_subtract_fusion.2
  249.9 1.1 fusion.151
  251.1 1.3 fusion.16
  252.4 1.4 fusion.14
  253.8 1.4 fusion.12
  255.1 1.4 fusion.10
  257.2 1.4 fusion.18
  258.6 1.5 collective-permute-start.6
  260.2 1.4 collective-permute-start.7
  261.7 2.3 collective-permute-start.9
  264.1 1.6 collective-permute-start.5
  265.6 117.0 %all-reduce.7.cloned.1.call-done = f32[64,512]{1,0:T(8,128)} async-done(((f32[64,512]{1,0:T(8,128)}), f32[64,512]{1,0:T(8,128)}) %all-reduce.7.cloned.1.call-update) | async-done | bytes 131088 | tf_op jit(solution)/shard_map/psum | solution.py:66
  382.6 1.3 fusion.66
  386.6 39.3 %psum.66 = f32[512]{0:T(512)S(1)} all-reduce(f32[512]{0:T(512)S(1)} %get-tuple-element.25), channel_id=1, replica_groups=mesh['hi'=4,'lo'=8] {'hi','lo'}, use_global_device_ids=true, to_apply=%region_8.9 | all-reduce | flops 512 | bytes 4096 | tf_op jit(solution)/shard_map/psum | solution.py:66
  426.1 31.2 %all_gather.10 = bf16[512,512]{1,0:T(8,128)(2,1)S(1)} all-gather(bf16[64,512]{1,0:T(8,128)(2,1)S(1)} %get-tuple-element.29), channel_id=1, replica_groups=mesh['hi'=4,'lo'=8] {'lo'}, dimensions={0}, use_global_device_ids=true | all-gather | bytes 589824 | tf_op jit(solution)/shard_map/all_gather | solution.py:82
  457.3 1.1 convolution_bitcast_fusion.1
  458.5 22.0 %reduce-scatter.6.cloned.1.call-done = f32[64,512]{1,0:T(8,128)} async-done(((f32[256,512]{1,0:T(8,128)}), f32[64,512]{1,0:T(8,128)}) %reduce-scatter.6.cloned.1.call-update) | async-done | bytes 131088 | tf_op jit(solution)/shard_map/reduce_scatter | solution.py:85
  480.5 2.2 multiply_reduce_fusion.2
  482.7 39.5 %psum.68 = f32[512]{0:T(512)S(1)} all-reduce(f32[512]{0:T(512)S(1)} %multiply_reduce_fusion.2), channel_id=1, replica_groups=mesh['hi'=4,'lo'=8] {'hi','lo'}, use_global_device_ids=true, to_apply=%region_13.14 | all-reduce | flops 512 | bytes 4096 | tf_op jit(solution)/shard_map/psum | solution.py:87
  522.2 2.2 multiply_subtract_fusion.1
  524.4 1.1 fusion.152
  525.6 1.3 fusion.6
  526.9 1.4 fusion.4
  528.2 1.4 fusion.2
  529.6 1.4 fusion
  531.7 1.4 fusion.8
  533.1 1.5 collective-permute-start.11
  534.7 1.4 collective-permute-start.12
  536.2 2.3 collective-permute-start.14
  538.5 1.5 collective-permute-start.10
  540.1 117.0 %all-reduce.9.cloned.1.call-done = f32[64,512]{1,0:T(8,128)} async-done(((f32[64,512]{1,0:T(8,128)}), f32[64,512]{1,0:T(8,128)}) %all-reduce.9.cloned.1.call-update) | async-done | bytes 131088 | tf_op jit(solution)/shard_map/psum | solution.py:66
  657.1 1.3 fusion.60
  660.2 0.8 multiply_reduce_fusion.1
  661.0 39.3 %psum.69 = f32[512]{0:T(512)S(1)} all-reduce(f32[512]{0:T(512)S(1)} %get-tuple-element.31), channel_id=1, replica_groups=mesh['hi'=4,'lo'=8] {'hi','lo'}, use_global_device_ids=true, to_apply=%region_15.16 | all-reduce | flops 512 | bytes 4096 | tf_op jit(solution)/shard_map/psum | solution.py:66
  700.6 31.2 %all_gather.11 = bf16[512,512]{1,0:T(8,128)(2,1)S(1)} all-gather(bf16[64,512]{1,0:T(8,128)(2,1)S(1)} %get-tuple-element.35), channel_id=1, replica_groups=mesh['hi'=4,'lo'=8] {'lo'}, dimensions={0}, use_global_device_ids=true | all-gather | bytes 589824 | tf_op jit(solution)/shard_map/all_gather | solution.py:82
  731.8 1.1 convolution_bitcast_fusion
  732.9 22.1 %reduce-scatter.8.cloned.1.call-done = f32[64,512]{1,0:T(8,128)} async-done(((f32[256,512]{1,0:T(8,128)}), f32[64,512]{1,0:T(8,128)}) %reduce-scatter.8.cloned.1.call-update) | async-done | bytes 131088 | tf_op jit(solution)/shard_map/reduce_scatter | solution.py:85
  755.1 2.2 multiply_reduce_fusion
  757.2 39.3 %psum.71 = f32[512]{0:T(512)S(1)} all-reduce(f32[512]{0:T(512)S(1)} %multiply_reduce_fusion), channel_id=1, replica_groups=mesh['hi'=4,'lo'=8] {'hi','lo'}, use_global_device_ids=true, to_apply=%region_20.21 | all-reduce | flops 512 | bytes 4096 | tf_op jit(solution)/shard_map/psum | solution.py:87
  796.6 2.9 multiply_subtract_fusion
  (110 shorter events, 14.3 us)
Async XLA Ops:
  7.2 176.8 %copy-start = (bf16[4,1,64,1,512]{4,2,3,1,0:T(8,128)(2,1)S(1)}, bf16[4,1,64,1,512]{4,2,3,1,0:T(8,128)(2,1)}, u32[]{:S(2)}) copy-start(bf16[4,1,64,1,512]{4,2,3,1,0:T(8,128)(2,1)} %param.8) | copy-start | bytes 786436
  7.2 141.2 %all-reduce.5.cloned.1.call-start = ((), (), s32[]{:S(2)}) async-start(), calls=%async_computation.3 | async-start | bytes 262144 | tf_op jit(solution)/shard_map/psum | solution.py:66
  12.1 137.5 %collective-permute-start.1 = (bf16[64,512]{1,0:T(8,128)(2,1)S(1)}, bf16[64,512]{1,0:T(8,128)(2,1)S(1)}, u32[]{:S(2)}, u32[]{:S(2)}) collective-permute-start(bf16[64,512]{1,0:T(8,128)(2,1)S(1)} %bitcast.372), channel_id=1, source_target_pairs={{0,2},{1,3},{2,0},{3,1},{4,6},{5,7},{6,4},{7,5},{8,10},{9,11},{10,... | collective-permute-start | bytes 196616 | tf_op jit(solution)/shard_map/ppermute | solution.py:12
  16.6 133.3 %collective-permute-start.2 = (bf16[64,512]{1,0:T(8,128)(2,1)S(1)}, bf16[64,512]{1,0:T(8,128)(2,1)S(1)}, u32[]{:S(2)}, u32[]{:S(2)}) collective-permute-start(bf16[64,512]{1,0:T(8,128)(2,1)S(1)} %bitcast.371), channel_id=1, source_target_pairs={{0,4},{1,5},{2,6},{3,7},{4,0},{5,1},{6,2},{7,3},{8,12},{9,13},{10,... | collective-permute-start | bytes 196616 | tf_op jit(solution)/shard_map/ppermute | solution.py:12
  20.7 129.5 %collective-permute-start.3 = (bf16[64,512]{1,0:T(8,128)(2,1)S(1)}, bf16[64,512]{1,0:T(8,128)(2,1)S(1)}, u32[]{:S(2)}, u32[]{:S(2)}) collective-permute-start(bf16[64,512]{1,0:T(8,128)(2,1)S(1)} %bitcast.370), channel_id=1, source_target_pairs={{0,8},{8,0},{16,24},{24,16},{1,9},{9,1},{17,25},{25,17},{2,10},{10... | collective-permute-start | bytes 196616 | tf_op jit(solution)/shard_map/ppermute | solution.py:12
  22.1 8.5 %copy-start.1 = (f32[9,64,64]{2,1,0:T(8,128)S(1)}, f32[9,64,64]{2,1,0:T(8,128)}, u32[]{:S(2)}) copy-start(f32[9,64,64]{2,1,0:T(8,128)} %param.12) | copy-start | bytes 442372
  22.1 128.4 %collective-permute-start.4 = (bf16[64,512]{1,0:T(8,128)(2,1)S(1)}, bf16[64,512]{1,0:T(8,128)(2,1)S(1)}, u32[]{:S(2)}, u32[]{:S(2)}) collective-permute-start(bf16[64,512]{1,0:T(8,128)(2,1)S(1)} %bitcast.368), channel_id=1, source_target_pairs={{0,16},{8,24},{16,0},{24,8},{1,17},{9,25},{17,1},{25,9},{2,18},{10... | collective-permute-start | bytes 196616 | tf_op jit(solution)/shard_map/ppermute | solution.py:12
  25.1 125.7 %collective-permute-start = (bf16[64,512]{1,0:T(8,128)(2,1)S(1)}, bf16[64,512]{1,0:T(8,128)(2,1)S(1)}, u32[]{:S(2)}, u32[]{:S(2)}) collective-permute-start(bf16[64,512]{1,0:T(8,128)(2,1)S(1)} %bitcast.369), channel_id=1, source_target_pairs={{0,1},{1,0},{2,3},{3,2},{4,5},{5,4},{6,7},{7,6},{8,9},{9,8},{10,11... | collective-permute-start | bytes 196616 | tf_op jit(solution)/shard_map/ppermute | solution.py:12
  27.4 178.7 %reduce-scatter.4.cloned.1.call-start = ((), (), s32[]{:S(2)}) async-start(), calls=%async_computation.4 | async-start | bytes 655360 | tf_op jit(solution)/shard_map/reduce_scatter | solution.py:85
  150.5 1.1 copy-start.2
  150.5 1.0 copy-start.3
  150.5 1.0 copy-start.5
  152.7 32.5 %copy-start.6 = (f32[2]{0:T(128)S(1)}, f32[2]{0:T(128)}, u32[]{:S(2)}) copy-start(f32[2]{0:T(128)} %param.14) | copy-start | bytes 28
  184.0 63.8 %copy-start.4 = (s32[512]{0:T(512)S(1)}, s32[512]{0:T(512)}, u32[]{:S(2)}) copy-start(s32[512]{0:T(512)} %param.15) | copy-start | bytes 6148
  185.1 197.5 %all-reduce.7.cloned.1.call-start = ((), (), s32[]{:S(2)}) async-start(), calls=%async_computation.5 | async-start | bytes 262144 | tf_op jit(solution)/shard_map/psum | solution.py:66
  257.2 223.3 %reduce-scatter.6.cloned.1.call-start = ((), (), s32[]{:S(2)}) async-start(), calls=%async_computation.6 | async-start | bytes 655360 | tf_op jit(solution)/shard_map/reduce_scatter | solution.py:85
  258.6 125.2 %collective-permute-start.6 = (bf16[64,512]{1,0:T(8,128)(2,1)S(1)}, bf16[64,512]{1,0:T(8,128)(2,1)S(1)}, u32[]{:S(2)}, u32[]{:S(2)}) collective-permute-start(bf16[64,512]{1,0:T(8,128)(2,1)S(1)} %bitcast.381), channel_id=1, source_target_pairs={{0,2},{1,3},{2,0},{3,1},{4,6},{5,7},{6,4},{7,5},{8,10},{9,11},{10,... | collective-permute-start | bytes 196616 | tf_op jit(solution)/shard_map/ppermute | solution.py:12
  260.2 124.0 %collective-permute-start.7 = (bf16[64,512]{1,0:T(8,128)(2,1)S(1)}, bf16[64,512]{1,0:T(8,128)(2,1)S(1)}, u32[]{:S(2)}, u32[]{:S(2)}) collective-permute-start(bf16[64,512]{1,0:T(8,128)(2,1)S(1)} %bitcast.380), channel_id=1, source_target_pairs={{0,4},{1,5},{2,6},{3,7},{4,0},{5,1},{6,2},{7,3},{8,12},{9,13},{10,... | collective-permute-start | bytes 196616 | tf_op jit(solution)/shard_map/ppermute | solution.py:12
  261.6 122.8 %collective-permute-start.8 = (bf16[64,512]{1,0:T(8,128)(2,1)S(1)}, bf16[64,512]{1,0:T(8,128)(2,1)S(1)}, u32[]{:S(2)}, u32[]{:S(2)}) collective-permute-start(bf16[64,512]{1,0:T(8,128)(2,1)S(1)} %bitcast.378), channel_id=1, source_target_pairs={{0,8},{8,0},{16,24},{24,16},{1,9},{9,1},{17,25},{25,17},{2,10},{10... | collective-permute-start | bytes 196616 | tf_op jit(solution)/shard_map/ppermute | solution.py:12
  261.7 123.0 %collective-permute-start.9 = (bf16[64,512]{1,0:T(8,128)(2,1)S(1)}, bf16[64,512]{1,0:T(8,128)(2,1)S(1)}, u32[]{:S(2)}, u32[]{:S(2)}) collective-permute-start(bf16[64,512]{1,0:T(8,128)(2,1)S(1)} %bitcast.376), channel_id=1, source_target_pairs={{0,16},{8,24},{16,0},{24,8},{1,17},{9,25},{17,1},{25,9},{2,18},{10... | collective-permute-start | bytes 196616 | tf_op jit(solution)/shard_map/ppermute | solution.py:12
  264.1 121.0 %collective-permute-start.5 = (bf16[64,512]{1,0:T(8,128)(2,1)S(1)}, bf16[64,512]{1,0:T(8,128)(2,1)S(1)}, u32[]{:S(2)}, u32[]{:S(2)}) collective-permute-start(bf16[64,512]{1,0:T(8,128)(2,1)S(1)} %bitcast.375), channel_id=1, source_target_pairs={{0,1},{1,0},{2,3},{3,2},{4,5},{5,4},{6,7},{7,6},{8,9},{9,8},{10,11... | collective-permute-start | bytes 196616 | tf_op jit(solution)/shard_map/ppermute | solution.py:12
  458.4 198.6 %all-reduce.9.cloned.1.call-start = ((), (), s32[]{:S(2)}) async-start(), calls=%async_computation.7 | async-start | bytes 262144 | tf_op jit(solution)/shard_map/psum | solution.py:66
  531.7 223.4 %reduce-scatter.8.cloned.1.call-start = ((), (), s32[]{:S(2)}) async-start(), calls=%async_computation.8 | async-start | bytes 655360 | tf_op jit(solution)/shard_map/reduce_scatter | solution.py:85
  533.1 125.2 %collective-permute-start.11 = (bf16[64,512]{1,0:T(8,128)(2,1)S(1)}, bf16[64,512]{1,0:T(8,128)(2,1)S(1)}, u32[]{:S(2)}, u32[]{:S(2)}) collective-permute-start(bf16[64,512]{1,0:T(8,128)(2,1)S(1)} %bitcast.382), channel_id=1, source_target_pairs={{0,2},{1,3},{2,0},{3,1},{4,6},{5,7},{6,4},{7,5},{8,10},{9,11},{10,... | collective-permute-start | bytes 196616 | tf_op jit(solution)/shard_map/ppermute | solution.py:12
  534.7 124.0 %collective-permute-start.12 = (bf16[64,512]{1,0:T(8,128)(2,1)S(1)}, bf16[64,512]{1,0:T(8,128)(2,1)S(1)}, u32[]{:S(2)}, u32[]{:S(2)}) collective-permute-start(bf16[64,512]{1,0:T(8,128)(2,1)S(1)} %bitcast.379), channel_id=1, source_target_pairs={{0,4},{1,5},{2,6},{3,7},{4,0},{5,1},{6,2},{7,3},{8,12},{9,13},{10,... | collective-permute-start | bytes 196616 | tf_op jit(solution)/shard_map/ppermute | solution.py:12
  536.1 122.8 %collective-permute-start.13 = (bf16[64,512]{1,0:T(8,128)(2,1)S(1)}, bf16[64,512]{1,0:T(8,128)(2,1)S(1)}, u32[]{:S(2)}, u32[]{:S(2)}) collective-permute-start(bf16[64,512]{1,0:T(8,128)(2,1)S(1)} %bitcast.377), channel_id=1, source_target_pairs={{0,8},{8,0},{16,24},{24,16},{1,9},{9,1},{17,25},{25,17},{2,10},{10... | collective-permute-start | bytes 196616 | tf_op jit(solution)/shard_map/ppermute | solution.py:12
  536.2 123.0 %collective-permute-start.14 = (bf16[64,512]{1,0:T(8,128)(2,1)S(1)}, bf16[64,512]{1,0:T(8,128)(2,1)S(1)}, u32[]{:S(2)}, u32[]{:S(2)}) collective-permute-start(bf16[64,512]{1,0:T(8,128)(2,1)S(1)} %bitcast.374), channel_id=1, source_target_pairs={{0,16},{8,24},{16,0},{24,8},{1,17},{9,25},{17,1},{25,9},{2,18},{10... | collective-permute-start | bytes 196616 | tf_op jit(solution)/shard_map/ppermute | solution.py:12
  538.5 120.9 %collective-permute-start.10 = (bf16[64,512]{1,0:T(8,128)(2,1)S(1)}, bf16[64,512]{1,0:T(8,128)(2,1)S(1)}, u32[]{:S(2)}, u32[]{:S(2)}) collective-permute-start(bf16[64,512]{1,0:T(8,128)(2,1)S(1)} %bitcast.373), channel_id=1, source_target_pairs={{0,1},{1,0},{2,3},{3,2},{4,5},{5,4},{6,7},{7,6},{8,9},{9,8},{10,11... | collective-permute-start | bytes 196616 | tf_op jit(solution)/shard_map/ppermute | solution.py:12
Sparse Core Ops, SparseCore 0:
  27.5 120.8 all-reduce.4
  185.2 20.8 reduce-scatter.3
  257.3 125.2 all-reduce.6
  458.6 21.9 reduce-scatter.5
  531.8 125.2 all-reduce.8
  733.1 21.9 reduce-scatter.7
where the time goes:
time: 808 us; the launch traced here: 806 us
  waiting for transfers between devices  411 us (51%)
  blocking collectives  291 us (36%)
  matrix products  43.6 us (5%)
  starting transfers between devices  23 us (3%)
  other arithmetic  18.3 us (2%)
  between operations  14.7 us (2%)
    psum x3, waiting for transfers between devices, precondition(): lax.psum((coefficients[level_total - 1], partial_energy), ('hi', 'lo'))  346 us
    psum x3, blocking collectives, precondition(): lax.psum((coefficients[level_total - 1], partial_energy), ('hi', 'lo'))  118 us
    all_gather x3, blocking collectives, local(): lax.all_gather(rounded, 'lo', axis=0, tiled=True)  93.7 us
    psum x2, blocking collectives, local(): curvature = lax.psum(jnp.sum(direction * image, axis=0), ('hi', 'lo'))  78.8 us
    reduce_scatter x3, waiting for transfers between devices, local(): lax.psum_scatter(partial_value, 'hi', scatter_dimension=0, tiled=True)  64.5 us
    ppermute x15, starting transfers between devices, from_partner(): return lax.ppermute(value, axis, pairs)  22.8 us
    dot_general x15, matrix products, level_pieces(): own_part = jnp.einsum('l,lrb->rb', select, coefficients)  20.4 us
  transfers between devices with their start and end apart: 21, of which 6 were waited for; matrix products, arithmetic and copies ran while one was open for 3% of the time, Pallas kernels for 0%

commit v1 on v0

--- a/solution.py
+++ b/solution.py
@@ -64,7 +64,7 @@
         coarse_basis = bases[:, split_at:]
         partial_energy = jnp.sum(resid * local_part, axis=0)
         total, summed_energy = lax.psum(
-            (coefficients[level_total - 1], partial_energy), ("hi", "lo")
+            lax.psum((coefficients[level_total - 1], partial_energy), "lo"), "hi"
         )
         coarse = jnp.dot(couplings[level_total - 1], total, precision=lax.Precision.HIGHEST)
         scaled = local_part + jnp.dot(coarse_basis, coarse, precision=lax.Precision.HIGHEST)

time: 808 us -> 673 us (0.83)
  waiting for transfers between devices: 411 us -> 281 us
    psum x3 -> x6, waiting for transfers between devices: 346 us -> 235 us  [the longest x3 188 us: precondition(): lax.psum((coefficients[level_total - 1], partial_energy), 'lo')]
    psum x3 -> x6, blocking collectives: 118 us -> 77.6 us  [the longest x3 60.3 us: precondition(): lax.psum((coefficients[level_total - 1], partial_energy), 'lo')]
    psum x2 -> x3, blocking collectives: 78.8 us -> 116 us  [local(): curvature = lax.psum(jnp.sum(direction * image, axis=0), ('hi', 'lo'))]
    reduce_scatter x3, waiting for transfers between devices: 64.5 us -> 43.2 us  [local(): lax.psum_scatter(partial_value, 'hi', scatter_dimension=0, tiled=True)]
  transfers between devices with their start and end apart: 21 -> 24, of which waited for: 6 -> 11; matrix products, arithmetic and copies ran while one was open for 3% -> 4% of each run, Pallas kernels for 0% -> 0%
where the time goes in v1:
time: 673 us; the launch traced here: 672 us
  blocking collectives  288 us (43%)
  waiting for transfers between devices  281 us (42%)
  matrix products  43.6 us (6%)
  starting transfers between devices  22.1 us (3%)
  other arithmetic  18.3 us (3%)
  between operations  14.4 us (2%)
    psum x3, waiting for transfers between devices, precondition(): lax.psum((coefficients[level_total - 1], partial_energy), 'lo')  188 us
    psum x3, blocking collectives, local(): curvature = lax.psum(jnp.sum(direction * image, axis=0), ('hi', 'lo'))  116 us
    all_gather x3, blocking collectives, local(): lax.all_gather(rounded, 'lo', axis=0, tiled=True)  94.2 us
    psum x3, blocking collectives, precondition(): lax.psum((coefficients[level_total - 1], partial_energy), 'lo')  60.3 us
    psum x3, waiting for transfers between devices, precondition(): lax.psum(lax.psum((coefficients[level_total - 1], partial_energy), 'lo'),...  46.4 us
    reduce_scatter x3, waiting for transfers between devices, local(): lax.psum_scatter(partial_value, 'hi', scatter_dimension=0, tiled=True)  43.2 us
    ppermute x15, starting transfers between devices, from_partner(): return lax.ppermute(value, axis, pairs)  21.7 us
    dot_general x15, matrix products, level_pieces(): own_part = jnp.einsum('l,lrb->rb', select, coefficients)  20.4 us
  transfers between devices with their start and end apart: 24, of which 11 were waited for; matrix products, arithmetic and copies ran while one was open for 4% of the time, Pallas kernels for 0%

profile of v1, /device:TPU:0, one launch (start us, length us, event | category | flops | bytes accessed | tf_op | source)
XLA Modules:
  0.0 671.9 jit_solution(17703400757043233605)
XLA Ops:
  7.2 1.5 fusion.146
  8.7 2.1 fusion.150
  10.8 1.3 fusion.26
  12.1 3.1 collective-permute-start.1
  15.3 1.4 fusion.24
  16.6 2.7 collective-permute-start.2
  19.3 1.4 fusion.22
  20.8 1.4 fusion.20
  22.1 1.6 collective-permute-start.4
  23.7 1.4 fusion.28
  25.1 1.6 collective-permute-start
  30.6 0.9 fusion.58
  31.5 0.9 fusion.54
  37.8 56.6 %all-reduce.7.cloned.1.call-done = f32[64,512]{1,0:T(8,128)} async-done(((f32[64,512]{1,0:T(8,128)}), f32[64,512]{1,0:T(8,128)}) %all-reduce.7.cloned.1.call-update) | async-done | bytes 131088 | tf_op jit(solution)/shard_map/psum | solution.py:67
  95.2 32.3 %all-reduce.9.cloned.1.call-done = f32[64,512]{1,0:T(8,128)} async-done(((f32[64,512]{1,0:T(8,128)}), f32[64,512]{1,0:T(8,128)}) %all-reduce.9.cloned.1.call-update) | async-done | bytes 131088 | tf_op jit(solution)/shard_map/psum | solution.py:66
  127.5 1.3 fusion.72
  129.1 31.4 %all_gather.9 = bf16[512,512]{1,0:T(8,128)(2,1)S(1)} all-gather(bf16[64,512]{1,0:T(8,128)(2,1)S(1)} %get-tuple-element.17), channel_id=1, replica_groups=mesh['hi'=4,'lo'=8] {'lo'}, dimensions={0}, use_global_device_ids=true | all-gather | bytes 589824 | tf_op jit(solution)/shard_map/all_gather | solution.py:82
  160.5 1.1 convolution_bitcast_fusion.2
  162.3 21.2 %psum.105 = f32[512]{0:T(512)S(1)} all-reduce(f32[512]{0:T(512)S(1)} %get-tuple-element.19), channel_id=1, replica_groups=mesh['hi'=4,'lo'=8] {'lo'}, use_global_device_ids=true, to_apply=%region_1.0 | all-reduce | flops 512 | bytes 4096 | tf_op jit(solution)/shard_map/psum | solution.py:67
  183.5 6.0 psum.106
  189.5 2.2 multiply_reduce_fusion.4
  191.6 37.0 %psum.109 = f32[512]{0:T(512)S(1)} all-reduce(f32[512]{0:T(512)S(1)} %multiply_reduce_fusion.4), channel_id=1, replica_groups=mesh['hi'=4,'lo'=8] {'hi','lo'}, use_global_device_ids=true, to_apply=%region_8.0 | all-reduce | flops 512 | bytes 4096 | tf_op jit(solution)/shard_map/psum | solution.py:87
  228.7 2.2 multiply_subtract_fusion.2
  230.9 1.1 fusion.151
  232.0 1.3 fusion.16
  233.3 1.4 fusion.14
  234.7 1.4 fusion.12
  236.0 1.4 fusion.10
  237.4 2.9 collective-permute-start.6
  240.3 1.4 fusion.18
  242.0 2.3 collective-permute-start.9
  245.7 1.4 collective-permute-done.7
  249.4 66.4 %all-reduce.11.cloned.1.call-done = f32[64,512]{1,0:T(8,128)} async-done(((f32[64,512]{1,0:T(8,128)}), f32[64,512]{1,0:T(8,128)}) %all-reduce.11.cloned.1.call-update) | async-done | bytes 131088 | tf_op jit(solution)/shard_map/psum | solution.py:67
  316.7 19.6 %psum.110 = f32[512]{0:T(512)S(1)} all-reduce(f32[512]{0:T(512)S(1)} %get-tuple-element.23), channel_id=1, replica_groups=mesh['hi'=4,'lo'=8] {'lo'}, use_global_device_ids=true, to_apply=%region_10.11 | all-reduce | flops 512 | bytes 4096 | tf_op jit(solution)/shard_map/psum | solution.py:67
  336.3 5.6 psum.111
  341.9 7.0 %all-reduce.13.cloned.1.call-done = f32[64,512]{1,0:T(8,128)} async-done(((f32[64,512]{1,0:T(8,128)}), f32[64,512]{1,0:T(8,128)}) %all-reduce.13.cloned.1.call-update) | async-done | bytes 131088 | tf_op jit(solution)/shard_map/psum | solution.py:66
  348.9 1.3 fusion.66
  350.4 31.4 %all_gather.10 = bf16[512,512]{1,0:T(8,128)(2,1)S(1)} all-gather(bf16[64,512]{1,0:T(8,128)(2,1)S(1)} %get-tuple-element.27), channel_id=1, replica_groups=mesh['hi'=4,'lo'=8] {'lo'}, dimensions={0}, use_global_device_ids=true | all-gather | bytes 589824 | tf_op jit(solution)/shard_map/all_gather | solution.py:82
  381.8 1.1 convolution_bitcast_fusion.1
  383.0 21.6 %reduce-scatter.6.cloned.1.call-done = f32[64,512]{1,0:T(8,128)} async-done(((f32[256,512]{1,0:T(8,128)}), f32[64,512]{1,0:T(8,128)}) %reduce-scatter.6.cloned.1.call-update) | async-done | bytes 131088 | tf_op jit(solution)/shard_map/reduce_scatter | solution.py:85
  404.6 2.2 multiply_reduce_fusion.2
  406.8 39.5 %psum.114 = f32[512]{0:T(512)S(1)} all-reduce(f32[512]{0:T(512)S(1)} %multiply_reduce_fusion.2), channel_id=1, replica_groups=mesh['hi'=4,'lo'=8] {'hi','lo'}, use_global_device_ids=true, to_apply=%region_17.18 | all-reduce | flops 512 | bytes 4096 | tf_op jit(solution)/shard_map/psum | solution.py:87
  446.3 2.2 multiply_subtract_fusion.1
  448.5 1.1 fusion.152
  449.6 1.3 fusion.6
  450.9 1.4 fusion.4
  452.3 1.4 fusion.2
  453.7 1.4 fusion
  455.0 1.5 collective-permute-start.11
  456.6 1.4 fusion.8
  458.0 1.4 collective-permute-start.12
  459.5 2.3 collective-permute-start.14
  461.8 1.5 collective-permute-start.10
  466.9 65.2 %all-reduce.15.cloned.1.call-done = f32[64,512]{1,0:T(8,128)} async-done(((f32[64,512]{1,0:T(8,128)}), f32[64,512]{1,0:T(8,128)}) %all-reduce.15.cloned.1.call-update) | async-done | bytes 131088 | tf_op jit(solution)/shard_map/psum | solution.py:67
  533.0 19.6 %psum.115 = f32[512]{0:T(512)S(1)} all-reduce(f32[512]{0:T(512)S(1)} %get-tuple-element.29), channel_id=1, replica_groups=mesh['hi'=4,'lo'=8] {'lo'}, use_global_device_ids=true, to_apply=%region_19.20 | all-reduce | flops 512 | bytes 4096 | tf_op jit(solution)/shard_map/psum | solution.py:67
  552.6 5.6 psum.116
  558.2 7.1 %all-reduce.17.cloned.1.call-done = f32[64,512]{1,0:T(8,128)} async-done(((f32[64,512]{1,0:T(8,128)}), f32[64,512]{1,0:T(8,128)}) %all-reduce.17.cloned.1.call-update) | async-done | bytes 131088 | tf_op jit(solution)/shard_map/psum | solution.py:66
  565.3 1.3 fusion.60
  566.9 31.4 %all_gather.11 = bf16[512,512]{1,0:T(8,128)(2,1)S(1)} all-gather(bf16[64,512]{1,0:T(8,128)(2,1)S(1)} %get-tuple-element.33), channel_id=1, replica_groups=mesh['hi'=4,'lo'=8] {'lo'}, dimensions={0}, use_global_device_ids=true | all-gather | bytes 589824 | tf_op jit(solution)/shard_map/all_gather | solution.py:82
  598.3 1.1 convolution_bitcast_fusion
  599.4 21.6 %reduce-scatter.8.cloned.1.call-done = f32[64,512]{1,0:T(8,128)} async-done(((f32[256,512]{1,0:T(8,128)}), f32[64,512]{1,0:T(8,128)}) %reduce-scatter.8.cloned.1.call-update) | async-done | bytes 131088 | tf_op jit(solution)/shard_map/reduce_scatter | solution.py:85
  621.0 2.2 multiply_reduce_fusion
  623.2 39.3 %psum.119 = f32[512]{0:T(512)S(1)} all-reduce(f32[512]{0:T(512)S(1)} %multiply_reduce_fusion), channel_id=1, replica_groups=mesh['hi'=4,'lo'=8] {'hi','lo'}, use_global_device_ids=true, to_apply=%region_26.27 | all-reduce | flops 512 | bytes 4096 | tf_op jit(solution)/shard_map/psum | solution.py:87
  662.5 2.9 multiply_subtract_fusion
  (123 shorter events, 20.9 us)
Async XLA Ops:
  7.2 153.3 %copy-start = (bf16[4,1,64,1,512]{4,2,3,1,0:T(8,128)(2,1)S(1)}, bf16[4,1,64,1,512]{4,2,3,1,0:T(8,128)(2,1)}, u32[]{:S(2)}) copy-start(bf16[4,1,64,1,512]{4,2,3,1,0:T(8,128)(2,1)} %param.8) | copy-start | bytes 786436
  7.2 87.1 %all-reduce.7.cloned.1.call-start = ((), (), s32[]{:S(2)}) async-start(), calls=%async_computation.3 | async-start | bytes 262144 | tf_op jit(solution)/shard_map/psum | solution.py:67
  12.1 23.7 %collective-permute-start.1 = (bf16[64,512]{1,0:T(8,128)(2,1)S(1)}, bf16[64,512]{1,0:T(8,128)(2,1)S(1)}, u32[]{:S(2)}, u32[]{:S(2)}) collective-permute-start(bf16[64,512]{1,0:T(8,128)(2,1)S(1)} %bitcast.372), channel_id=1, source_target_pairs={{0,2},{1,3},{2,0},{3,1},{4,6},{5,7},{6,4},{7,5},{8,10},{9,11},{10,... | collective-permute-start | bytes 196616 | tf_op jit(solution)/shard_map/ppermute | solution.py:12
  16.6 19.5 %collective-permute-start.2 = (bf16[64,512]{1,0:T(8,128)(2,1)S(1)}, bf16[64,512]{1,0:T(8,128)(2,1)S(1)}, u32[]{:S(2)}, u32[]{:S(2)}) collective-permute-start(bf16[64,512]{1,0:T(8,128)(2,1)S(1)} %bitcast.371), channel_id=1, source_target_pairs={{0,4},{1,5},{2,6},{3,7},{4,0},{5,1},{6,2},{7,3},{8,12},{9,13},{10,... | collective-permute-start | bytes 196616 | tf_op jit(solution)/shard_map/ppermute | solution.py:12
  20.7 15.8 %collective-permute-start.3 = (bf16[64,512]{1,0:T(8,128)(2,1)S(1)}, bf16[64,512]{1,0:T(8,128)(2,1)S(1)}, u32[]{:S(2)}, u32[]{:S(2)}) collective-permute-start(bf16[64,512]{1,0:T(8,128)(2,1)S(1)} %bitcast.370), channel_id=1, source_target_pairs={{0,8},{8,0},{16,24},{24,16},{1,9},{9,1},{17,25},{25,17},{2,10},{10... | collective-permute-start | bytes 196616 | tf_op jit(solution)/shard_map/ppermute | solution.py:12
  22.1 8.5 %copy-start.1 = (f32[9,64,64]{2,1,0:T(8,128)S(1)}, f32[9,64,64]{2,1,0:T(8,128)}, u32[]{:S(2)}) copy-start(f32[9,64,64]{2,1,0:T(8,128)} %param.12) | copy-start | bytes 442372
  22.1 14.6 %collective-permute-start.4 = (bf16[64,512]{1,0:T(8,128)(2,1)S(1)}, bf16[64,512]{1,0:T(8,128)(2,1)S(1)}, u32[]{:S(2)}, u32[]{:S(2)}) collective-permute-start(bf16[64,512]{1,0:T(8,128)(2,1)S(1)} %bitcast.368), channel_id=1, source_target_pairs={{0,16},{8,24},{16,0},{24,8},{1,17},{9,25},{17,1},{25,9},{2,18},{10... | collective-permute-start | bytes 196616 | tf_op jit(solution)/shard_map/ppermute | solution.py:12
  25.1 11.9 %collective-permute-start = (bf16[64,512]{1,0:T(8,128)(2,1)S(1)}, bf16[64,512]{1,0:T(8,128)(2,1)S(1)}, u32[]{:S(2)}, u32[]{:S(2)}) collective-permute-start(bf16[64,512]{1,0:T(8,128)(2,1)S(1)} %bitcast.369), channel_id=1, source_target_pairs={{0,1},{1,0},{2,3},{3,2},{4,5},{5,4},{6,7},{7,6},{8,9},{9,8},{10,11... | collective-permute-start | bytes 196616 | tf_op jit(solution)/shard_map/ppermute | solution.py:12
  27.4 100.2 %all-reduce.9.cloned.1.call-start = ((), (), s32[]{:S(2)}) async-start(), calls=%async_computation.4 | async-start | bytes 262144 | tf_op jit(solution)/shard_map/psum | solution.py:66
  37.0 57.4 %copy-start.2 = (f32[64,576]{1,0:T(8,128)S(1)}, f32[64,576]{1,0:T(8,128)}, u32[]{:S(2)}) copy-start(f32[64,576]{1,0:T(8,128)} %param.11) | copy-start | bytes 442372
  37.0 57.4 %copy-start.3 = (f32[64,512]{1,0:T(8,128)S(1)}, f32[64,512]{1,0:T(8,128)}, u32[]{:S(2)}) copy-start(f32[64,512]{1,0:T(8,128)} %param.9) | copy-start | bytes 393220
  37.0 57.4 %copy-start.5 = (f32[64]{0:T(128)S(1)}, f32[64]{0:T(128)}, u32[]{:S(2)}) copy-start(f32[64]{0:T(128)} %param.10) | copy-start | bytes 772
  94.4 95.1 %reduce-scatter.4.cloned.1.call-start = ((), (), s32[]{:S(2)}) async-start(), calls=%async_computation.5 | async-start | bytes 655360 | tf_op jit(solution)/shard_map/reduce_scatter | solution.py:85
  129.1 32.6 %copy-start.6 = (f32[2]{0:T(128)S(1)}, f32[2]{0:T(128)}, u32[]{:S(2)}) copy-start(f32[2]{0:T(128)} %param.14) | copy-start | bytes 28
  160.5 68.2 %copy-start.4 = (s32[512]{0:T(512)S(1)}, s32[512]{0:T(512)}, u32[]{:S(2)}) copy-start(s32[512]{0:T(512)} %param.15) | copy-start | bytes 6148
  161.6 154.2 %all-reduce.11.cloned.1.call-start = ((), (), s32[]{:S(2)}) async-start(), calls=%async_computation.6 | async-start | bytes 262144 | tf_op jit(solution)/shard_map/psum | solution.py:67
  237.4 8.0 %collective-permute-start.6 = (bf16[64,512]{1,0:T(8,128)(2,1)S(1)}, bf16[64,512]{1,0:T(8,128)(2,1)S(1)}, u32[]{:S(2)}, u32[]{:S(2)}) collective-permute-start(bf16[64,512]{1,0:T(8,128)(2,1)S(1)} %bitcast.382), channel_id=1, source_target_pairs={{0,2},{1,3},{2,0},{3,1},{4,6},{5,7},{6,4},{7,5},{8,10},{9,11},{10,... | collective-permute-start | bytes 196616 | tf_op jit(solution)/shard_map/ppermute | solution.py:12
  241.7 5.4 collective-permute-start.7
  241.9 5.5 collective-permute-start.8
  242.0 5.7 collective-permute-start.9
  244.4 4.3 collective-permute-start.5
  245.4 103.5 %all-reduce.13.cloned.1.call-start = ((), (), s32[]{:S(2)}) async-start(), calls=%async_computation.7 | async-start | bytes 262144 | tf_op jit(solution)/shard_map/psum | solution.py:66
  315.8 88.7 %reduce-scatter.6.cloned.1.call-start = ((), (), s32[]{:S(2)}) async-start(), calls=%async_computation.8 | async-start | bytes 655360 | tf_op jit(solution)/shard_map/reduce_scatter | solution.py:85
  382.9 149.2 %all-reduce.15.cloned.1.call-start = ((), (), s32[]{:S(2)}) async-start(), calls=%async_computation.9 | async-start | bytes 262144 | tf_op jit(solution)/shard_map/psum | solution.py:67
  455.0 9.1 %collective-permute-start.11 = (bf16[64,512]{1,0:T(8,128)(2,1)S(1)}, bf16[64,512]{1,0:T(8,128)(2,1)S(1)}, u32[]{:S(2)}, u32[]{:S(2)}) collective-permute-start(bf16[64,512]{1,0:T(8,128)(2,1)S(1)} %bitcast.381), channel_id=1, source_target_pairs={{0,2},{1,3},{2,0},{3,1},{4,6},{5,7},{6,4},{7,5},{8,10},{9,11},{10,... | collective-permute-start | bytes 196616 | tf_op jit(solution)/shard_map/ppermute | solution.py:12
  458.0 6.4 collective-permute-start.12
  459.4 5.3 collective-permute-start.13
  459.5 5.5 collective-permute-start.14
  461.8 4.3 collective-permute-start.10
  464.1 101.3 %all-reduce.17.cloned.1.call-start = ((), (), s32[]{:S(2)}) async-start(), calls=%async_computation.10 | async-start | bytes 262144 | tf_op jit(solution)/shard_map/psum | solution.py:66
  532.1 88.9 %reduce-scatter.8.cloned.1.call-start = ((), (), s32[]{:S(2)}) async-start(), calls=%async_computation.11 | async-start | bytes 655360 | tf_op jit(solution)/shard_map/reduce_scatter | solution.py:85
Sparse Core Ops, SparseCore 0:
  27.5 66.7 all-reduce.6
  96.6 30.8 all-reduce.8
  161.7 21.4 reduce-scatter.3
  245.5 70.2 all-reduce.10
  318.0 30.8 all-reduce.12
  383.1 21.4 reduce-scatter.5
  464.2 67.8 all-reduce.14
  534.4 30.8 all-reduce.16
  599.5 21.4 reduce-scatter.7
